TPU v7x, 32 devices: a whole 2x2x4 slice. The times are simulated.
32 devices in a mesh: expert: 4 (over x, core), dp: 8 (over z, y).
Axes of the slice: x: 2, y: 2, z: 4, core: 2. Of those that a mesh axis runs over, the one named last changes fastest.
Arguments:
- tokens: bfloat16 [4096, 1024], P(('expert', 'dp')), may hold values from -6 to 6
- norm_gain: float32 [1024], replicated, may hold values from 0.1 to 1.9
- router_weight: bfloat16 [1024, 4], replicated, may hold values from -0.3984375 to 0.3984375
- shared_gate_vector: float32 [1024], replicated, may hold values from -0.4 to 0.4
- expert_ids: int32 [4096, 2], P(('expert', 'dp')), may hold values from 0 to 3, all different within a row; in each aligned block of 128 rows (0 to 127, 128 to 255, ...) at most 96 rows name the same one
- gate_weight: bfloat16 [4, 1024, 4096], P('expert', None, 'dp'), may hold values from -0.1875 to 0.1875
- up_weight: bfloat16 [4, 1024, 4096], P('expert', None, 'dp'), may hold values from -0.1875 to 0.1875
- down_weight: bfloat16 [4, 1024, 4096], P('expert', None, 'dp'), may hold values from -0.09375 to 0.09375
- shared_gate_weight: bfloat16 [1024, 4096], P(None, 'expert'), may hold values from -0.1875 to 0.1875
- shared_up_weight: bfloat16 [1024, 4096], P(None, 'expert'), may hold values from -0.1875 to 0.1875
- shared_down_weight: bfloat16 [4096, 1024], P('expert'), may hold values from -0.09375 to 0.09375
Outputs:
- mixed: bfloat16 [4096, 1024], P(('expert', 'dp'))
Inputs may be any that keep to these rules, and one draw needn't show every extreme that they name: `expert_ids`: in each aligned block of 128 rows (the rows of one device) no expert is named by more than 96 pairs, and in some block one expert is named by exactly 96; the two ids of a row differ.
All inputs are finite; a program needn't handle non-finite values.
Results may differ from a plain program's by a relative error of at most 0.0085.
Values may be sent and summed in bfloat16 or wider, within the bound.
A program may use at most 128 MiB of HBM per device.

v0:
```python
import functools

import jax
import jax.numpy as jnp
from jax import lax
from jax.experimental import pallas as pl
from jax.experimental.pallas import tpu as pltpu
from jax.sharding import PartitionSpec as P


def rms_norm(values, gain):
    floats = values.astype(jnp.float32)
    mean_square = jnp.mean(floats * floats, axis=-1, keepdims=True)
    return (floats * lax.rsqrt(mean_square + 1e-06) * gain).astype(jnp.bfloat16)


def routing(normed, router_weight, expert_ids):
    logits = jnp.dot(normed, router_weight, preferred_element_type=jnp.float32)
    onehot = (
        expert_ids[:, :, None] == jnp.arange(router_weight.shape[1], dtype=jnp.int32)[None, None, :]
    )
    picked = jnp.sum(jnp.where(onehot, logits[:, None, :], jnp.float32(0.0)), axis=-1)
    first_weight = jax.nn.sigmoid(picked[:, 0] - picked[:, 1])
    return jnp.stack([first_weight, 1.0 - first_weight], axis=1)


def slot_of(block_ids, experts):
    flat_ids = block_ids.reshape(-1)
    onehot = (flat_ids[:, None] == jnp.arange(experts, dtype=jnp.int32)[None, :]).astype(jnp.int32)
    before = jnp.cumsum(onehot, axis=0) - onehot
    return jnp.sum(before * onehot, axis=1).reshape(block_ids.shape)


def swiglu_hidden(inputs, gate_piece, up_piece):
    gate_part = jnp.dot(inputs, gate_piece, preferred_element_type=jnp.float32)
    up_part = jnp.dot(inputs, up_piece, preferred_element_type=jnp.float32)
    return (jax.nn.silu(gate_part) * up_part).astype(jnp.bfloat16)


def down_product(hidden, down_piece):
    return lax.dot_general(
        hidden, down_piece, (((1,), (1,)), ((), ())), preferred_element_type=jnp.float32
    )


def body(
    tokens,
    norm_gain,
    router_weight,
    shared_gate_vector,
    expert_ids,
    gate_weight,
    up_weight,
    down_weight,
    shared_gate_weight,
    shared_up_weight,
    shared_down_weight,
):
    experts = lax.axis_size("expert")
    tok_rows = tokens.shape[0]
    width = tokens.shape[1]
    capacity = 3 * tok_rows // experts
    normed = rms_norm(tokens, norm_gain)
    route_weight = routing(normed, router_weight, expert_ids)
    slot = slot_of(expert_ids, experts)
    target = expert_ids * capacity + slot
    slot_iota = jnp.arange(experts * capacity, dtype=jnp.int32)[:, None]
    dispatch_table = (
        (target[:, 0][None, :] == slot_iota) | (target[:, 1][None, :] == slot_iota)
    ).astype(jnp.bfloat16)
    outgoing = jnp.dot(dispatch_table, normed, preferred_element_type=jnp.float32).astype(
        jnp.bfloat16
    )
    outgoing = outgoing.reshape(experts, capacity, width)
    arrived = lax.all_to_all(outgoing, "expert", split_axis=0, concat_axis=0, tiled=True).reshape(
        experts * capacity, width
    )
    hidden = swiglu_hidden(
        arrived,
        lax.all_gather(gate_weight, "dp", axis=2, tiled=True)[0],
        lax.all_gather(up_weight, "dp", axis=2, tiled=True)[0],
    )
    hidden_all = hidden
    hidden = hidden_all
    expert_out = down_product(hidden, lax.all_gather(down_weight, "dp", axis=2, tiled=True)[0])
    expert_out = expert_out.astype(jnp.bfloat16).reshape(experts, capacity, width)
    returned_rows = lax.all_to_all(
        expert_out, "expert", split_axis=0, concat_axis=0, tiled=True
    ).reshape(experts * capacity, width)
    fetched = returned_rows[target].astype(jnp.float32)
    routed = jnp.sum(route_weight[:, :, None] * fetched, axis=1)
    gathered = lax.all_gather(normed, "expert", axis=0, tiled=True)
    hidden = swiglu_hidden(gathered, shared_gate_weight, shared_up_weight)
    shared = lax.psum_scatter(
        jnp.dot(hidden, shared_down_weight, preferred_element_type=jnp.float32).astype(
            jnp.bfloat16
        ),
        "expert",
        scatter_dimension=0,
        tiled=True,
    ).astype(jnp.float32)
    shared_gate = jax.nn.sigmoid(jnp.sum(normed.astype(jnp.float32) * shared_gate_vector, axis=-1))
    return (routed + shared_gate[:, None] * shared).astype(jnp.bfloat16)

NONE, X, Y, XY = 0, 1, 2, 3
Z0, Z1, Z2, Z12 = 0, 1, 2, 3
VMEM_LIMIT = 62 * 1024 * 1024


def flipped(position, bit):
    return position + bit - 2 * bit * ((position // bit) % 2)


def fused_kernel(
    rows,
    hidden_units,
    shared_units,
    tokens_ref,
    gain_ref,
    router_ref,
    vector_ref,
    ids_ref,
    gate_ref,
    up_ref,
    down_ref,
    sgate_ref,
    sup_ref,
    sdown_ref,
    out_ref,
    tok,
    sc,
    part,
    from_core,
    from_diag,
    from_x,
    from_y,
    from_z,
    w_gate,
    w_up,
    down_raw,
    w_down,
    send_sem,
    recv_sem,
    load_sem,
):
    e_at = lax.axis_index("expert")
    d_at = lax.axis_index("dp")
    partner = {
        "c": (flipped(e_at, 1), d_at),
        "x": (flipped(e_at, 2), d_at),
        "y": (e_at, flipped(d_at, 1)),
        "z1": (e_at, flipped(d_at, 2)),
        "z2": (e_at, flipped(d_at, 4)),
    }
    half = rows // 2
    messages = {}

    def send(name, src, dst, to):
        at = len(messages)
        copy = pltpu.make_async_remote_copy(
            src_ref=src,
            dst_ref=dst,
            send_sem=send_sem.at[at],
            recv_sem=recv_sem.at[at],
            device_id=partner[to],
            device_id_type=pl.DeviceIdType.MESH,
        )
        copy.start()
        messages[name] = copy

    def arrive(name):
        messages[name].wait_recv()

    first = pl.multiple_of(d_at * shared_units, shared_units)
    loads = [
        pltpu.make_async_copy(gate_ref.at[0], w_gate.at[:, pl.ds(0, hidden_units)], load_sem.at[0]),
        pltpu.make_async_copy(up_ref.at[0], w_up.at[:, pl.ds(0, hidden_units)], load_sem.at[1]),
        pltpu.make_async_copy(
            sgate_ref.at[:, pl.ds(first, shared_units)],
            w_gate.at[:, pl.ds(hidden_units, shared_units)],
            load_sem.at[2],
        ),
        pltpu.make_async_copy(
            sup_ref.at[:, pl.ds(first, shared_units)],
            w_up.at[:, pl.ds(hidden_units, shared_units)],
            load_sem.at[3],
        ),
        pltpu.make_async_copy(
            sdown_ref.at[pl.ds(first, shared_units), :],
            w_down.at[pl.ds(hidden_units, shared_units), :],
            load_sem.at[4],
        ),
        pltpu.make_async_copy(down_ref.at[0], down_raw, load_sem.at[5]),
    ]
    for load in loads:
        load.start()

    barrier = pltpu.get_barrier_semaphore()
    for to in partner.values():
        pl.semaphore_signal(
            barrier, inc=1, device_id=to, device_id_type=pl.DeviceIdType.MESH
        )

    floats = tokens_ref[...].astype(jnp.float32)
    mean_square = jnp.mean(floats * floats, axis=-1, keepdims=True)
    normed = (floats * lax.rsqrt(mean_square + 1e-06) * gain_ref[...][None, :]).astype(jnp.bfloat16)
    tok[0, 0] = normed
    logits = jnp.dot(normed, router_ref[...], preferred_element_type=jnp.float32)
    ids = ids_ref[...]
    first_id, second_id = ids[:, 0:1], ids[:, 1:2]
    column = lax.broadcasted_iota(jnp.int32, logits.shape, 1)
    margin = jnp.sum(
        jnp.where(column == first_id, logits, 0.0), axis=1, keepdims=True
    ) - jnp.sum(jnp.where(column == second_id, logits, 0.0), axis=1, keepdims=True)
    first_weight = jax.nn.sigmoid(margin)
    shared_gate = jax.nn.sigmoid(
        jnp.sum(normed.astype(jnp.float32) * vector_ref[...][None, :], axis=-1, keepdims=True)
    )
    column = lax.broadcasted_iota(jnp.int32, (rows, sc.shape[2]), 1)
    scales = jnp.where(column == first_id, first_weight, 0.0)
    scales = scales + jnp.where(column == second_id, 1.0 - first_weight, 0.0)
    scales = scales + jnp.where(column == sc.shape[2] - 1, shared_gate, 0.0)
    sc[0, 0] = jnp.transpose(scales)
    pl.semaphore_wait(barrier, len(partner))

    def slot(z, xy):
        return 4 * z + xy

    def send_tokens(kind, z_from, xy_from, z_to, xy_to, to):
        send((kind, z_to, xy_to), tok.at[slot(z_from, xy_from), 0], tok.at[slot(z_to, xy_to), 0], to)
        send(
            (kind + "s", z_to, xy_to), sc.at[slot(z_from, xy_from), 0], sc.at[slot(z_to, xy_to), 0], to
        )

    def tokens_arrive(kind, z, xy):
        arrive((kind, z, xy))
        arrive((kind + "s", z, xy))

    def share(z, xy):
        at = slot(z, xy)
        send(("c", z, xy), tok.at[at, 0], tok.at[at, 1], "c")
        send(("cs", z, xy), sc.at[at, 0], sc.at[at, 1], "c")

    def spread(z):
        send_tokens("g", z, NONE, z, X, "x")
        send_tokens("g", z, NONE, z, Y, "y")
        share(z, NONE)

    def diagonal(z):
        tokens_arrive("g", z, X)
        tokens_arrive("g", z, Y)
        low, high = pl.ds(0, half), pl.ds(half, half)
        send(
            ("lo", z), tok.at[slot(z, Y), 0, low], tok.at[slot(z, XY), 0, low], "x"
        )
        send(
            ("hi", z), tok.at[slot(z, X), 0, high], tok.at[slot(z, XY), 0, high], "y"
        )
        send(("ds", z), sc.at[slot(z, X), 0], sc.at[slot(z, XY), 0], "y")
        share(z, X)
        share(z, Y)

    def diagonal_arrives(z):
        arrive(("lo", z))
        arrive(("hi", z))
        arrive(("ds", z))
        share(z, XY)

    def compute(z, xy):
        arrive(("c", z, xy))
        arrive(("cs", z, xy))
        at = slot(z, xy)
        lane = lax.broadcasted_iota(jnp.int32, (rows, sc.shape[2]), 1)
        routed_scale, shared_scale = [], []
        for core in range(2):
            columns = jnp.transpose(sc[at, core])
            routed_scale.append(
                jnp.sum(jnp.where(lane == e_at, columns, 0.0), axis=1, keepdims=True)
            )
            shared_scale.append(columns[:, sc.shape[2] - 1 :])
        routed_scale = jnp.concatenate(routed_scale, axis=0)
        shared_scale = jnp.concatenate(shared_scale, axis=0)
        inputs = tok[at].reshape(2 * rows, tok.shape[3])
        gate_part = jnp.dot(inputs, w_gate[...], preferred_element_type=jnp.float32)
        up_part = jnp.dot(inputs, w_up[...], preferred_element_type=jnp.float32)
        hidden = gate_part * jax.nn.sigmoid(gate_part) * up_part
        hidden = jnp.concatenate(
            [
                (hidden[:, :hidden_units] * routed_scale).astype(jnp.bfloat16),
                (hidden[:, hidden_units:] * shared_scale).astype(jnp.bfloat16),
            ],
            axis=1,
        )
        result = jnp.dot(hidden, w_down[...], preferred_element_type=jnp.float32)
        part[at] = result.astype(jnp.bfloat16).reshape(2, rows, tok.shape[3])
        send(("pc", z, xy), part.at[at, 1], from_core.at[at], "c")

    def f32(values):
        return values.astype(jnp.float32)

    def chip_sum(z, xy):
        arrive(("pc", z, xy))
        return f32(part[slot(z, xy), 0]) + f32(from_core[slot(z, xy)])

    def send_diagonal(z):
        at = slot(z, XY)
        part[at, 0] = chip_sum(z, XY).astype(jnp.bfloat16)
        low, high = pl.ds(0, half), pl.ds(half, half)
        send(("plo", z), part.at[at, 0, low], from_diag.at[z, low], "x")
        send(("phi", z), part.at[at, 0, high], from_diag.at[z, high], "y")

    def send_sides(z):
        arrive(("plo", z))
        arrive(("phi", z))
        total = chip_sum(z, X)
        part[slot(z, X), 0, :half] = total[:half].astype(jnp.bfloat16)
        part[slot(z, X), 0, half:] = (total[half:] + f32(from_diag[z, half:])).astype(jnp.bfloat16)
        send(("px", z), part.at[slot(z, X), 0], from_x.at[z], "x")
        total = chip_sum(z, Y)
        part[slot(z, Y), 0, :half] = (total[:half] + f32(from_diag[z, :half])).astype(jnp.bfloat16)
        part[slot(z, Y), 0, half:] = total[half:].astype(jnp.bfloat16)
        send(("py", z), part.at[slot(z, Y), 0], from_y.at[z], "y")

    def column_sum(z):
        total = chip_sum(z, NONE)
        arrive(("px", z))
        arrive(("py", z))
        return total + f32(from_x[z]) + f32(from_y[z])

    send_tokens("g", Z0, NONE, Z1, NONE, "z1")
    spread(Z0)
    send_tokens("g", Z0, NONE, Z2, NONE, "z2")
    for load in loads:
        load.wait()
    w_down[0:hidden_units, :] = jnp.transpose(down_raw[...])

    order = (Z0, Z1, Z2, Z12)
    for number, z in enumerate(order):
        compute(z, NONE)
        diagonal(z)
        if number + 1 < len(order):
            later = order[number + 1]
            tokens_arrive("g", later, NONE)
            if later == Z2:
                send_tokens("g", Z2, NONE, Z12, NONE, "z1")
            spread(later)
        compute(z, X)
        compute(z, Y)
        diagonal_arrives(z)
        compute(z, XY)
        if number:
            send_diagonal(order[number - 1])
    send_diagonal(Z12)

    send_sides(Z12)
    send_sides(Z2)
    part[slot(Z12, NONE), 0] = column_sum(Z12).astype(jnp.bfloat16)
    send(("pz", Z12), part.at[slot(Z12, NONE), 0], from_z.at[0], "z1")
    send_sides(Z1)
    total = column_sum(Z2)
    arrive(("pz", Z12))
    part[slot(Z2, NONE), 0] = (total + f32(from_z[0])).astype(jnp.bfloat16)
    send(("pz", Z2), part.at[slot(Z2, NONE), 0], from_z.at[1], "z2")
    send_sides(Z0)
    part[slot(Z1, NONE), 0] = column_sum(Z1).astype(jnp.bfloat16)
    send(("pz", Z1), part.at[slot(Z1, NONE), 0], from_z.at[2], "z1")
    total = column_sum(Z0)
    arrive(("pz", Z2))
    arrive(("pz", Z1))
    out_ref[...] = (total + f32(from_z[1]) + f32(from_z[2])).astype(out_ref.dtype)
    for copy in messages.values():
        copy.wait_send()


MESSAGES = 112


def fused_body(
    tokens,
    norm_gain,
    router_weight,
    shared_gate_vector,
    expert_ids,
    gate_weight,
    up_weight,
    down_weight,
    shared_gate_weight,
    shared_up_weight,
    shared_down_weight,
):
    rows, width = tokens.shape
    hidden_units = gate_weight.shape[2]
    shared_units = shared_gate_weight.shape[1] // lax.axis_size("dp")
    units = hidden_units + shared_units
    planes = 16
    anywhere = pl.BlockSpec(memory_space=pl.ANY)
    block = (rows, width)
    return pl.pallas_call(
        functools.partial(fused_kernel, rows, hidden_units, shared_units),
        out_shape=jax.ShapeDtypeStruct(block, jnp.bfloat16),
        in_specs=[pl.BlockSpec(memory_space=pltpu.VMEM)] * 5 + [anywhere] * 6,
        out_specs=pl.BlockSpec(memory_space=pltpu.VMEM),
        scratch_shapes=[
            pltpu.VMEM((planes, 2) + block, jnp.bfloat16),
            pltpu.VMEM((planes, 2, 8, rows), jnp.float32),
            pltpu.VMEM((planes, 2) + block, jnp.bfloat16),
            pltpu.VMEM((planes,) + block, jnp.bfloat16),
            pltpu.VMEM((4,) + block, jnp.bfloat16),
            pltpu.VMEM((4,) + block, jnp.bfloat16),
            pltpu.VMEM((4,) + block, jnp.bfloat16),
            pltpu.VMEM((3,) + block, jnp.bfloat16),
            pltpu.VMEM((width, units), jnp.bfloat16),
            pltpu.VMEM((width, units), jnp.bfloat16),
            pltpu.VMEM((width, hidden_units), jnp.bfloat16),
            pltpu.VMEM((units, width), jnp.bfloat16),
            pltpu.SemaphoreType.DMA((MESSAGES,)),
            pltpu.SemaphoreType.DMA((MESSAGES,)),
            pltpu.SemaphoreType.DMA((6,)),
        ],
        compiler_params=pltpu.CompilerParams(
            collective_id=0, has_side_effects=True, vmem_limit_bytes=VMEM_LIMIT
        ),
    )(
        tokens,
        norm_gain,
        router_weight,
        shared_gate_vector,
        expert_ids,
        gate_weight,
        up_weight,
        down_weight,
        shared_gate_weight,
        shared_up_weight,
        shared_down_weight,
    )


def solution(mesh):
    fused = (mesh.shape["expert"], mesh.shape["dp"]) == (1 << 2, 1 << 3)
    return jax.shard_map(
        fused_body if fused else body,
        mesh=mesh,
        in_specs=(
            P(("expert", "dp"), None),
            P(),
            P(),
            P(),
            P(("expert", "dp"), None),
            P("expert", None, "dp"),
            P("expert", None, "dp"),
            P("expert", None, "dp"),
            P(None, "expert"),
            P(None, "expert"),
            P("expert", None),
        ),
        out_specs=P(("expert", "dp"), None),
        check_vma=False,
    )
```

profile of v0, /device:TPU:0, one launch (start us, length us, event | category | flops | bytes accessed | tf_op | source)
XLA Modules:
  0.0 99.6 jit_solution(11162376505255430208)
XLA Ops:
  0.0 1.4 %copy.13.ids_ref = s32[128,2]{1,0:T(8,128)} copy(s32[128,2]{0,1:T(2,128)} %param.15) | data formatting | bytes 2048 | tf_op args[4]
  1.4 1.6 %copy.12.router_ref = bf16[1024,4]{1,0:T(8,128)(2,1)} copy(bf16[1024,4]{0,1:T(4,128)(2,1)} %param.13) | data formatting | bytes 16384 | tf_op args[2]
  3.0 95.0 %shard_map.109 = bf16[128,1024]{1,0:T(8,128)(2,1)} custom-call(bf16[128,1024]{1,0:T(8,128)(2,1)} %tokens_ref.1, f32[1024]{0:T(1024)} %gain_ref.1, bf16[1024,4]{1,0:T(8,128)(2,1)} %copy.12.router_ref, f32[1024]{0:T(1024)} %vector_ref.1, s32[128,2]{1,0:T(8,128)} %copy.13.ids_ref, bf16[1,1024,512]{2,1,0:T(8,128)(2,1)} %gate_ref.1, ...), custom_call_target="tpu_custom_call" | custom-call | tf_op jit(solution)/shard_map/pallas_call | solution.py:398
  98.0 1.7 %copy.15 = bf16[128,1024]{1,0:T(8,128)(2,1)} copy(bf16[128,1024]{1,0:T(8,128)(2,1)} %shard_map.109) | data formatting | bytes 524288
where the time goes:
time: 99.9 us; the launch traced here: 99.6 us
  Pallas kernels  95 us (95%)
  local copies, waits for them, and re-layouts  4.65 us (5%)
    pallas_call x1, Pallas kernels, fused_body(): pl.pallas_call(functools.partial(fused_kernel, rows, hidden_units, shared...  95 us
    unnamed x3, local copies, waits for them, and re-layouts  4.65 us

commit v1 on v0

v1 whole, which is shorter than its diff:
```python
import functools

import jax
import jax.numpy as jnp
from jax import lax
from jax.experimental import pallas as pl
from jax.experimental.pallas import tpu as pltpu
from jax.sharding import PartitionSpec as P


def rms_norm(values, gain):
    floats = values.astype(jnp.float32)
    mean_square = jnp.mean(floats * floats, axis=-1, keepdims=True)
    return (floats * lax.rsqrt(mean_square + 1e-06) * gain).astype(jnp.bfloat16)


def routing(normed, router_weight, expert_ids):
    logits = jnp.dot(normed, router_weight, preferred_element_type=jnp.float32)
    onehot = (
        expert_ids[:, :, None] == jnp.arange(router_weight.shape[1], dtype=jnp.int32)[None, None, :]
    )
    picked = jnp.sum(jnp.where(onehot, logits[:, None, :], jnp.float32(0.0)), axis=-1)
    first_weight = jax.nn.sigmoid(picked[:, 0] - picked[:, 1])
    return jnp.stack([first_weight, 1.0 - first_weight], axis=1)


def slot_of(block_ids, experts):
    flat_ids = block_ids.reshape(-1)
    onehot = (flat_ids[:, None] == jnp.arange(experts, dtype=jnp.int32)[None, :]).astype(jnp.int32)
    before = jnp.cumsum(onehot, axis=0) - onehot
    return jnp.sum(before * onehot, axis=1).reshape(block_ids.shape)


def swiglu_hidden(inputs, gate_piece, up_piece):
    gate_part = jnp.dot(inputs, gate_piece, preferred_element_type=jnp.float32)
    up_part = jnp.dot(inputs, up_piece, preferred_element_type=jnp.float32)
    return (jax.nn.silu(gate_part) * up_part).astype(jnp.bfloat16)


def down_product(hidden, down_piece):
    return lax.dot_general(
        hidden, down_piece, (((1,), (1,)), ((), ())), preferred_element_type=jnp.float32
    )


def body(
    tokens,
    norm_gain,
    router_weight,
    shared_gate_vector,
    expert_ids,
    gate_weight,
    up_weight,
    down_weight,
    shared_gate_weight,
    shared_up_weight,
    shared_down_weight,
):
    experts = lax.axis_size("expert")
    tok_rows = tokens.shape[0]
    width = tokens.shape[1]
    capacity = 3 * tok_rows // experts
    normed = rms_norm(tokens, norm_gain)
    route_weight = routing(normed, router_weight, expert_ids)
    slot = slot_of(expert_ids, experts)
    target = expert_ids * capacity + slot
    slot_iota = jnp.arange(experts * capacity, dtype=jnp.int32)[:, None]
    dispatch_table = (
        (target[:, 0][None, :] == slot_iota) | (target[:, 1][None, :] == slot_iota)
    ).astype(jnp.bfloat16)
    outgoing = jnp.dot(dispatch_table, normed, preferred_element_type=jnp.float32).astype(
        jnp.bfloat16
    )
    outgoing = outgoing.reshape(experts, capacity, width)
    arrived = lax.all_to_all(outgoing, "expert", split_axis=0, concat_axis=0, tiled=True).reshape(
        experts * capacity, width
    )
    hidden = swiglu_hidden(
        arrived,
        lax.all_gather(gate_weight, "dp", axis=2, tiled=True)[0],
        lax.all_gather(up_weight, "dp", axis=2, tiled=True)[0],
    )
    hidden_all = hidden
    hidden = hidden_all
    expert_out = down_product(hidden, lax.all_gather(down_weight, "dp", axis=2, tiled=True)[0])
    expert_out = expert_out.astype(jnp.bfloat16).reshape(experts, capacity, width)
    returned_rows = lax.all_to_all(
        expert_out, "expert", split_axis=0, concat_axis=0, tiled=True
    ).reshape(experts * capacity, width)
    fetched = returned_rows[target].astype(jnp.float32)
    routed = jnp.sum(route_weight[:, :, None] * fetched, axis=1)
    gathered = lax.all_gather(normed, "expert", axis=0, tiled=True)
    hidden = swiglu_hidden(gathered, shared_gate_weight, shared_up_weight)
    shared = lax.psum_scatter(
        jnp.dot(hidden, shared_down_weight, preferred_element_type=jnp.float32).astype(
            jnp.bfloat16
        ),
        "expert",
        scatter_dimension=0,
        tiled=True,
    ).astype(jnp.float32)
    shared_gate = jax.nn.sigmoid(jnp.sum(normed.astype(jnp.float32) * shared_gate_vector, axis=-1))
    return (routed + shared_gate[:, None] * shared).astype(jnp.bfloat16)

MESH = pl.DeviceIdType.MESH
NONE, X, Y, XY = 0, 1, 2, 3
END, MID = 0, 1
VMEM_LIMIT = 62 * 1024 * 1024
SEMAPHORES = 192
LEAD_SHARE = 6
ANCHORS = ("S", "W", "CP", "CQ")


def operations(role):
    ops = [("S",), ("W",), ("sc", "c"), ("sc", "x"), ("sc", "y")]
    travels = [("in", 0)] if role == 0 else [("out", 1), ("in", 1), ("in", 0), ("out", 2), ("out", 3)]
    returns = [("rin", 1), ("rin", 2), ("rin", 3)] if role == 0 else [("rout", 0), ("rin", 2), ("rin", 3)]
    ops += [("sc",) + way for way in travels]
    ops += [("P",) + way + (half,) for way in travels + returns for half in range(2)]
    for plane in range(4):
        ops += [
            ("P", step, plane, half) for step in ("x", "y", "sx", "sy", "px", "py", "col") for half in range(2)
        ]
        ops += [("P", step, plane) for step in ("lo", "hi", "d", "plo", "phi")]
        ops += [(kind, *step, plane, at) for kind, *step in (("P", "c"), ("CP",), ("P", "pc")) for at in range(4)]
        ops += [(kind, *step, plane, pair) for kind, *step in (("CQ",), ("Q", "pc")) for pair in range(2)]
        ops += [("Q", "c", plane, at) for at in range(4)]
        if plane != role:
            ops += [("Q", "col", plane, at) for at in range(4)]
    ops += [("Q",) + way + (at,) for way in travels + returns for at in range(4)]
    ops += [("Q", step) for step in ("x", "y", "lo", "hi", "d", "plo", "phi", "sx", "px", "sy", "py", "end")]
    return ops


ORDER_END = (
    6, 198, 199, 49, 33, 0, 7, 2, 16, 15, 1, 200, 3, 201, 184, 55, 51, 53, 50, 183, 29, 72, 54,
    182, 52, 45, 4, 185, 67, 47, 37, 98, 41, 115, 97, 73, 68, 5, 46, 139, 48, 141, 133, 110, 111,
    75, 158, 140, 142, 176, 153, 134, 99, 118, 177, 96, 159, 154, 160, 171, 173, 175, 163, 167,
    117, 28, 56, 181, 174, 197, 180, 164, 168, 196, 143, 147, 116, 128, 161, 90, 130, 17, 170,
    172, 146, 122, 91, 126, 150, 74, 14, 36, 138, 193, 179, 131, 137, 178, 165, 169, 132, 195, 35,
    112, 113, 114, 40, 192, 44, 155, 157, 156, 34, 85, 87, 88, 194, 127, 129, 89, 30, 31, 32, 95,
    189, 94, 162, 166, 188, 136, 202, 135, 84, 191, 86, 203, 204, 144, 148, 145, 149, 79, 83, 190,
    93, 92, 121, 125, 186, 69, 70, 71, 207, 205, 120, 124, 208, 206, 187, 152, 151, 102, 103, 119,
    13, 106, 123, 100, 104, 101, 77, 12, 105, 107, 81, 78, 82, 209, 76, 80, 108, 10, 57, 61, 58,
    59, 63, 60, 39, 62, 64, 43, 109, 11, 38, 42, 20, 21, 24, 65, 8, 18, 22, 19, 23, 25, 66, 9, 26,
    27,
)
ORDER_MID = (
    12, 227, 226, 10, 104, 88, 0, 2, 13, 11, 71, 70, 1, 14, 16, 3, 228, 229, 28, 26, 106, 105,
    200, 110, 127, 45, 17, 27, 100, 15, 63, 107, 102, 92, 18, 4, 153, 109, 62, 96, 204, 145, 61,
    208, 40, 46, 41, 201, 170, 64, 19, 101, 205, 152, 103, 123, 188, 203, 212, 58, 7, 165, 209,
    154, 146, 48, 60, 50, 202, 189, 213, 54, 49, 6, 166, 122, 187, 198, 53, 57, 9, 211, 59, 30,
    151, 172, 84, 183, 199, 186, 185, 52, 210, 173, 130, 83, 29, 56, 176, 8, 196, 143, 180, 177,
    181, 171, 197, 108, 111, 144, 42, 158, 140, 142, 167, 206, 182, 168, 169, 184, 91, 47, 134,
    207, 138, 193, 225, 128, 69, 72, 129, 139, 5, 141, 192, 194, 224, 124, 175, 179, 162, 195, 43,
    157, 68, 132, 136, 217, 150, 221, 155, 161, 159, 89, 90, 156, 67, 133, 216, 137, 191, 223,
    112, 94, 160, 44, 98, 149, 220, 115, 174, 178, 119, 125, 66, 215, 190, 222, 76, 51, 55, 230,
    131, 126, 231, 34, 135, 31, 32, 33, 65, 214, 93, 232, 97, 148, 35, 219, 36, 114, 95, 99, 147,
    218, 113, 235, 73, 118, 116, 85, 233, 37, 117, 164, 25, 87, 86, 163, 24, 236, 234, 39, 21,
    120, 22, 80, 77, 74, 75, 38, 20, 121, 23, 79, 78, 237, 81, 82,
)


def flipped(position, bit):
    return position + bit - 2 * bit * ((position // bit) % 2)


def halves(count, number):
    half = count // 2 // 16 * 16
    if 2 * half == count or number in (1, 2):
        return half
    return count - half


def target(role, op):
    kind, step, rest = op[0], op[1], op[2:]
    if step in ("in", "out"):
        plane, more = rest[0], rest[1:]
        if step == "out":
            return "out", END, (kind, "z", plane) + more
        return "in", MID, (kind, "z", plane if role == END else 3 - plane) + more
    if step == "rin":
        plane, more = rest[0], rest[1:]
        if role == END:
            return "in", MID, (kind, "rz", 1, plane) + more
        return "in", MID, (kind, "rz", 0, 3 - plane) + more
    if step == "rout":
        return "out", END, (kind, "rz", 0) + rest
    if step in ("c", "pc"):
        return "c", role, op
    return ("x" if step in ("x", "lo", "plo", "px") else "y"), role, op


def fused_kernel(
    rows,
    lead,
    hidden_units,
    shared_units,
    tokens_ref,
    gain_ref,
    router_ref,
    vector_ref,
    ids_ref,
    gate_ref,
    up_ref,
    down_ref,
    sgate_ref,
    sup_ref,
    sdown_ref,
    out_ref,
    sc,
    tok_p,
    tok_q,
    part_p,
    part_q,
    core_p,
    core_q,
    diag_p,
    diag_q,
    x_p,
    x_q,
    y_p,
    y_q,
    line_p,
    line_q,
    w_gate,
    w_up,
    down_raw,
    w_down,
    send_sem,
    recv_sem,
    load_sem,
):
    e_at = lax.axis_index("expert")
    d_at = lax.axis_index("dp")
    rest = rows - lead
    z_at = d_at // 2
    toward = 2 * (1 - 2 * (z_at // 2))
    mid = (z_at + z_at // 2) % 2
    partner = {
        "c": (flipped(e_at, 1), d_at),
        "x": (flipped(e_at, 2), d_at),
        "y": (e_at, flipped(d_at, 1)),
        "in": (e_at, d_at + toward),
        "out": (e_at, d_at - toward),
    }
    barrier = pltpu.get_barrier_semaphore()
    for to in ("c", "x", "y", "in"):
        pl.semaphore_signal(barrier, inc=1, device_id=partner[to], device_id_type=MESH)

    @pl.when(mid == 1)
    def _():
        pl.semaphore_signal(barrier, inc=1, device_id=partner["out"], device_id_type=MESH)

    first = pl.multiple_of(d_at * shared_units, shared_units)
    loads = [
        pltpu.make_async_copy(gate_ref.at[0], w_gate.at[:, pl.ds(0, hidden_units)], load_sem.at[0]),
        pltpu.make_async_copy(up_ref.at[0], w_up.at[:, pl.ds(0, hidden_units)], load_sem.at[1]),
        pltpu.make_async_copy(
            sgate_ref.at[:, pl.ds(first, shared_units)],
            w_gate.at[:, pl.ds(hidden_units, shared_units)],
            load_sem.at[2],
        ),
        pltpu.make_async_copy(
            sup_ref.at[:, pl.ds(first, shared_units)],
            w_up.at[:, pl.ds(hidden_units, shared_units)],
            load_sem.at[3],
        ),
        pltpu.make_async_copy(
            sdown_ref.at[pl.ds(first, shared_units), :],
            w_down.at[pl.ds(hidden_units, shared_units), :],
            load_sem.at[4],
        ),
        pltpu.make_async_copy(down_ref.at[0], down_raw, load_sem.at[5]),
    ]
    for load in loads:
        load.start()

    floats = tokens_ref[...].astype(jnp.float32)
    mean_square = jnp.mean(floats * floats, axis=-1, keepdims=True)
    normed = (floats * lax.rsqrt(mean_square + 1e-06) * gain_ref[...][None, :]).astype(jnp.bfloat16)
    tok_p[mid, NONE, 0] = normed[:lead]
    tok_q[mid, NONE, 0] = normed[lead:]
    pl.semaphore_wait(barrier, 4 + mid)

    lines = sc.shape[3]
    def make_scales():
        normed = jnp.concatenate([tok_p[mid, NONE, 0], tok_q[mid, NONE, 0]], axis=0)
        logits = lax.dot_general(
            router_ref[...], normed, (((1,), (1,)), ((), ())), preferred_element_type=jnp.float32
        )
        ids = ids_ref[...]
        first_id, second_id = ids[0:1], ids[1:2]
        row = lax.broadcasted_iota(jnp.int32, logits.shape, 0)
        margin = jnp.sum(
            jnp.where(row == first_id, logits, 0.0), axis=0, keepdims=True
        ) - jnp.sum(jnp.where(row == second_id, logits, 0.0), axis=0, keepdims=True)
        first_weight = jax.nn.sigmoid(margin)
        shared_gate = jax.nn.sigmoid(
            jnp.sum(normed.astype(jnp.float32) * vector_ref[...][None, :], axis=-1, keepdims=True)
        )
        column = lax.broadcasted_iota(jnp.int32, (rows, lines), 1)
        row = lax.broadcasted_iota(jnp.int32, (lines, rows), 0)
        scales = jnp.transpose(jnp.where(column == lines - 1, shared_gate, 0.0))
        scales = scales + jnp.where(row == first_id, first_weight, 0.0)
        scales = scales + jnp.where(row == second_id, 1.0 - first_weight, 0.0)
        sc[mid, NONE, 0] = scales

    numbers = {}

    def number(name):
        return numbers.setdefault(name, len(numbers))

    def landing(role, name):
        kind, step = name[0], name[1]
        if kind == "sc":
            if step == "z":
                return sc.at[name[2]]
            return {"c": sc.at[role, NONE, 1], "x": sc.at[role, X], "y": sc.at[role, pl.ds(2, 2)]}[step]
        if kind == "P":
            plane = name[3] if step == "rz" else name[2]
            at = halves(lead, plane)
            low, high = pl.ds(0, at), pl.ds(at, lead - at)
            if step == "rz":
                return line_p.at[name[2], plane, high if name[4] else low]
            if step == "c":
                return tok_p.at[plane, name[3], 1]
            if step == "pc":
                return core_p.at[plane, name[3]]
            if step in ("z", "x", "y"):
                place = {"z": NONE, "x": X, "y": Y}[step]
                return tok_p.at[plane, place, 0, high if name[3] else low]
            if step in ("px", "py"):
                return (x_p if step == "px" else y_p).at[plane, high if name[3] else low]
            return {
                "lo": tok_p.at[plane, XY, 0, low],
                "hi": tok_p.at[plane, XY, 0, high],
                "plo": diag_p.at[plane, low],
                "phi": diag_p.at[plane, high],
            }[step]
        at = halves(rest, role)
        low, high = pl.ds(0, at), pl.ds(at, rest - at)
        if step == "rz":
            return line_q.at[name[2], name[3], name[4]]
        if step == "z":
            return tok_q.at[name[2], name[3], 0]
        if step == "c":
            return tok_q.at[name[2], name[3], 1]
        if step == "pc":
            return core_q.at[name[2], pl.ds(2 * name[3], 2)]
        return {
            "x": tok_q.at[role, X, 0],
            "y": tok_q.at[role, Y, 0],
            "lo": tok_q.at[role, XY, 0, low],
            "hi": tok_q.at[role, XY, 0, high],
            "plo": diag_q.at[low],
            "phi": diag_q.at[high],
            "px": x_q,
            "py": y_q,
        }[step]

    def source(role, op):
        kind, step = op[0], op[1]
        if kind == "sc":
            if step in ("in", "out"):
                return sc.at[op[2]]
            return {"c": sc.at[role, NONE, 0], "x": sc.at[role, NONE], "y": sc.at[role, pl.ds(0, 2)]}[
                step
            ]
        if kind == "P":
            plane = op[2]
            at = halves(lead, plane)
            low, high = pl.ds(0, at), pl.ds(at, lead - at)
            if step == "c":
                return tok_p.at[plane, op[3], 0]
            if step == "pc":
                return part_p.at[plane, op[3], 1]
            if step in ("in", "out", "x", "y"):
                return tok_p.at[plane, NONE, 0, high if op[3] else low]
            if step in ("px", "py", "rin", "rout"):
                place = {"px": X, "py": Y}.get(step, NONE)
                return part_p.at[plane, place, 0, high if op[3] else low]
            return {
                "lo": tok_p.at[plane, Y, 0, low],
                "hi": tok_p.at[plane, X, 0, high],
                "plo": part_p.at[plane, XY, 0, low],
                "phi": part_p.at[plane, XY, 0, high],
            }[step]
        at = halves(rest, role)
        low, high = pl.ds(0, at), pl.ds(at, rest - at)
        if step in ("in", "out", "c"):
            return tok_q.at[op[2], op[3], 0]
        if step == "pc":
            return part_q.at[op[2], pl.ds(2 * op[3], 2), 1]
        if step in ("rin", "rout"):
            return part_q.at[op[2], op[3], 0]
        return {
            "x": tok_q.at[role, NONE, 0],
            "y": tok_q.at[role, NONE, 0],
            "lo": tok_q.at[role, Y, 0, low],
            "hi": tok_q.at[role, X, 0, high],
            "plo": part_q.at[role, XY, 0, low],
            "phi": part_q.at[role, XY, 0, high],
            "px": part_q.at[role, X, 0],
            "py": part_q.at[role, Y, 0],
        }[step]

    arrived = set()
    sent = {END: [], MID: []}

    def arrive(role, *names):
        for name in names:
            if (role, name) in arrived:
                continue
            arrived.add((role, name))
            ref = landing(role, name)
            pltpu.make_async_remote_copy(
                src_ref=ref,
                dst_ref=ref,
                send_sem=send_sem.at[0],
                recv_sem=recv_sem.at[number(name)],
                device_id=partner["c"],
                device_id_type=MESH,
            ).wait_recv()

    def block_here(role, kind, plane, at):
        if kind == "Q":
            if plane != role:
                return [("Q", "z", plane, at)]
            return {
                NONE: [],
                X: [("Q", "x")],
                Y: [("Q", "y")],
                XY: [("Q", "lo"), ("Q", "hi")],
            }[at]
        if at == XY:
            return [("P", "lo", plane), ("P", "hi", plane)]
        if at == NONE and plane == role:
            return []
        return [("P", ("z", "x", "y")[at], plane, part) for part in range(2)]

    def scales_here(role, plane, at):
        if plane != role:
            return [("sc", "z", plane)]
        return [[("sc", "c")], [("sc", "x")], [("sc", "y")], [("sc", "y")]][at]

    def needs(role, op):
        kind, step = op[0], op[1]
        if kind == "sc":
            if step in ("in", "out"):
                return scales_here(role, op[2], XY)
            return {"c": [], "x": [("sc", "c")], "y": [("sc", "x")]}[step]
        if step == "c":
            return block_here(role, kind, op[2], op[3])
        if step == "lo":
            return [("P", "y", op[2], 0)] if kind == "P" else [("Q", "y")]
        if step == "hi":
            return [("P", "x", op[2], 1)] if kind == "P" else [("Q", "x")]
        if step in ("in", "out", "x", "y"):
            if kind == "P":
                return [] if op[2] == role else [("P", "z", op[2], op[3])]
            return block_here(role, kind, op[2], op[3]) if step in ("in", "out") else []
        return []

    def copy_of(role, op, at):
        link, _, name = target(role, op)
        there = END if link == "out" else MID if link == "in" else role
        return pltpu.make_async_remote_copy(
            src_ref=source(role, op),
            dst_ref=landing(there, name),
            send_sem=send_sem.at[at],
            recv_sem=recv_sem.at[number(name)],
            device_id=partner[link],
            device_id_type=MESH,
        )

    def send(role, op):
        arrive(role, *needs(role, op))
        copy_of(role, op, len(sent[role])).start()
        sent[role].append(op)

    def f32(values):
        return values.astype(jnp.float32)

    def sides(role, plane):
        if role == plane:
            return (0,) if role == END else (1, 0)
        if role == END:
            return ()
        return (0,) if plane == END else (1,)

    def bf16(values):
        return values.astype(jnp.bfloat16)

    def chip_p(role, plane, at, span):
        arrive(role, ("P", "pc", plane, at))
        return f32(part_p[plane, at, 0, span]) + f32(core_p[plane, at, span])

    def chip_q(role, plane, at):
        arrive(role, ("Q", "pc", plane, at // 2))
        total = f32(part_q[plane, at, 0]) + f32(core_q[plane, at])
        for side in sides(role, plane):
            arrive(role, ("Q", "rz", side, plane, at))
            total = total + f32(line_q[side, plane, at])
        return total

    def add_p(role, step, plane, part=None):
        cut = halves(lead, plane)
        span = slice(cut, lead) if part else slice(0, cut)
        if step == "d":
            part_p[plane, XY, 0] = bf16(chip_p(role, plane, XY, slice(0, lead)))
        elif step in ("sx", "sy"):
            at = X if step == "sx" else Y
            total = chip_p(role, plane, at, span)
            if part == (1 if step == "sx" else 0):
                arrive(role, ("P", "phi" if step == "sx" else "plo", plane))
                total = total + f32(diag_p[plane, span])
            part_p[plane, at, 0, span] = bf16(total)
        else:
            total = chip_p(role, plane, NONE, span)
            arrive(role, ("P", "px", plane, part), ("P", "py", plane, part))
            total = total + f32(x_p[plane, span]) + f32(y_p[plane, span])
            for side in sides(role, plane):
                arrive(role, ("P", "rz", side, plane, part))
                total = total + f32(line_p[side, plane, span])
            if plane == role:
                out_ref[span] = total.astype(out_ref.dtype)
            else:
                part_p[plane, NONE, 0, span] = bf16(total)

    def add_q(role, step, *more):
        cut = halves(rest, role)
        if step == "col":
            plane, at = more
            part_q[plane, at, 0] = bf16(chip_q(role, plane, at))
        elif step == "d":
            part_q[role, XY, 0] = bf16(chip_q(role, role, XY))
        elif step == "sx":
            total = chip_q(role, role, X)
            arrive(role, ("Q", "phi"))
            part_q[role, X, 0, :cut] = bf16(total[:cut])
            part_q[role, X, 0, cut:] = bf16(total[cut:] + f32(diag_q[cut:]))
        elif step == "sy":
            total = chip_q(role, role, Y)
            arrive(role, ("Q", "plo"))
            part_q[role, Y, 0, :cut] = bf16(total[:cut] + f32(diag_q[:cut]))
            part_q[role, Y, 0, cut:] = bf16(total[cut:])
        else:
            total = chip_q(role, role, NONE)
            arrive(role, ("Q", "px"), ("Q", "py"))
            out_ref[lead:] = (total + f32(x_q[...]) + f32(y_q[...])).astype(out_ref.dtype)

    def scale_columns(blocks, low, high):
        line = lax.broadcasted_iota(jnp.int32, (high - low, lines), 1)
        routed, shared = [], []
        for block in blocks:
            columns = jnp.transpose(block)[low:high]
            routed.append(jnp.sum(jnp.where(line == e_at, columns, 0.0), axis=1, keepdims=True))
            shared.append(columns[:, lines - 1 :])
        return jnp.concatenate(routed, axis=0), jnp.concatenate(shared, axis=0)

    def experts(inputs, scales):
        routed_scale, shared_scale = scales
        gate_part = jnp.dot(inputs, w_gate[...], preferred_element_type=jnp.float32)
        up_part = jnp.dot(inputs, w_up[...], preferred_element_type=jnp.float32)
        hidden = gate_part * jax.nn.sigmoid(gate_part) * up_part
        hidden = jnp.concatenate(
            [
                bf16(hidden[:, :hidden_units] * routed_scale),
                bf16(hidden[:, hidden_units:] * shared_scale),
            ],
            axis=1,
        )
        return bf16(jnp.dot(hidden, w_down[...], preferred_element_type=jnp.float32))

    def by_role(at_end, at_mid):
        return at_end if at_end == at_mid else at_end + (at_mid - at_end) * mid

    def compute(op_end, op_mid):
        plane, at = by_role(op_end[1], op_mid[1]), by_role(op_end[2], op_mid[2])
        width = tok_p.shape[4]
        if op_end[0] == "CP":
            inputs = tok_p[plane, at].reshape(2 * lead, width)
            blocks = [sc[plane, at, core] for core in range(2)]
            result = experts(inputs, scale_columns(blocks, 0, lead))
            part_p[plane, at] = result.reshape(2, lead, width)
        else:
            pair = pl.ds(2 * at, 2)
            inputs = tok_q[plane, pair].reshape(4 * rest, width)
            blocks = [sc[plane, 2 * at + one, core] for one in range(2) for core in range(2)]
            result = experts(inputs, scale_columns(blocks, lead, rows))
            part_q[plane, pair] = result.reshape(2, 2, rest, width)

    def ready(role, op):
        plane, at = op[1], op[2]
        if op[0] == "CP":
            arrive(role, *block_here(role, "P", plane, at), ("P", "c", plane, at))
            arrive(role, *scales_here(role, plane, at))
        else:
            for one in (2 * at, 2 * at + 1):
                arrive(role, *block_here(role, "Q", plane, one), ("Q", "c", plane, one))
                arrive(role, *scales_here(role, plane, one))

    def anchors(role, order):
        parts, ops = [[]], operations(role)
        for op in (ops[at] for at in order):
            parts[-1].append(op)
            if op[0] in ANCHORS:
                parts.append([])
        return parts

    def run(role, part):
        for op in part:
            if op[0] in ("S", "W"):
                continue
            if op[0] in ("CP", "CQ"):
                ready(role, op)
            elif op[0] == "P" and op[1] in ("d", "sx", "sy", "col"):
                add_p(role, *op[1:])
            elif op[0] == "Q" and op[1] in ("d", "sx", "sy", "col", "end"):
                add_q(role, *op[1:])
            else:
                send(role, op)

    for part_end, part_mid in zip(anchors(END, ORDER_END), anchors(MID, ORDER_MID), strict=True):

        @pl.when(mid == 0)
        def _():
            run(END, part_end)

        @pl.when(mid == 1)
        def _():
            run(MID, part_mid)

        if not part_end or part_end[-1][0] not in ANCHORS:
            continue
        if part_end[-1][0] == "S":
            make_scales()
        elif part_end[-1][0] == "W":
            for load in loads:
                load.wait()
            w_down[0:hidden_units, :] = jnp.transpose(down_raw[...])
        else:
            compute(part_end[-1], part_mid[-1])

    @pl.when(mid == 0)
    def _():
        for at, op in enumerate(sent[END]):
            copy_of(END, op, at).wait_send()

    @pl.when(mid == 1)
    def _():
        for at, op in enumerate(sent[MID]):
            copy_of(MID, op, at).wait_send()


def fused_body(
    tokens,
    norm_gain,
    router_weight,
    shared_gate_vector,
    expert_ids,
    gate_weight,
    up_weight,
    down_weight,
    shared_gate_weight,
    shared_up_weight,
    shared_down_weight,
):
    rows, width = tokens.shape
    hidden_units = gate_weight.shape[2]
    shared_units = shared_gate_weight.shape[1] // lax.axis_size("dp")
    units = hidden_units + shared_units
    lead = LEAD_SHARE * rows // 8
    rest = rows - lead
    anywhere = pl.BlockSpec(memory_space=pl.ANY)

    def blocks(count, *planes):
        return pltpu.VMEM(planes + (count, width), jnp.bfloat16)

    return pl.pallas_call(
        functools.partial(fused_kernel, rows, lead, hidden_units, shared_units),
        out_shape=jax.ShapeDtypeStruct((rows, width), jnp.bfloat16),
        in_specs=[pl.BlockSpec(memory_space=pltpu.VMEM)] * 5 + [anywhere] * 6,
        out_specs=pl.BlockSpec(memory_space=pltpu.VMEM),
        scratch_shapes=[
            pltpu.VMEM((4, 4, 2, 8, rows), jnp.float32),
            blocks(lead, 4, 4, 2),
            blocks(rest, 4, 4, 2),
            blocks(lead, 4, 4, 2),
            blocks(rest, 4, 4, 2),
            blocks(lead, 4, 4),
            blocks(rest, 4, 4),
            blocks(lead, 4),
            blocks(rest),
            blocks(lead, 4),
            blocks(rest),
            blocks(lead, 4),
            blocks(rest),
            blocks(lead, 2, 4),
            blocks(rest, 2, 4, 4),
            pltpu.VMEM((width, units), jnp.bfloat16),
            pltpu.VMEM((width, units), jnp.bfloat16),
            pltpu.VMEM((width, hidden_units), jnp.bfloat16),
            pltpu.VMEM((units, width), jnp.bfloat16),
            pltpu.SemaphoreType.DMA((SEMAPHORES,)),
            pltpu.SemaphoreType.DMA((SEMAPHORES,)),
            pltpu.SemaphoreType.DMA((6,)),
        ],
        compiler_params=pltpu.CompilerParams(
            collective_id=0, has_side_effects=True, vmem_limit_bytes=VMEM_LIMIT
        ),
    )(
        tokens,
        norm_gain,
        router_weight.T,
        shared_gate_vector,
        expert_ids.T,
        gate_weight,
        up_weight,
        down_weight,
        shared_gate_weight,
        shared_up_weight,
        shared_down_weight,
    )


def solution(mesh):
    fused = (mesh.shape["expert"], mesh.shape["dp"]) == (1 << 2, 1 << 3)
    return jax.shard_map(
        fused_body if fused else body,
        mesh=mesh,
        in_specs=(
            P(("expert", "dp"), None),
            P(),
            P(),
            P(),
            P(("expert", "dp"), None),
            P("expert", None, "dp"),
            P("expert", None, "dp"),
            P("expert", None, "dp"),
            P(None, "expert"),
            P(None, "expert"),
            P("expert", None),
        ),
        out_specs=P(("expert", "dp"), None),
        check_vma=False,
    )
```

time: 99.9 us -> 73.2 us (0.73)
  Pallas kernels: 95 us -> 71.3 us
  local copies, waits for them, and re-layouts: 4.65 us -> 1.67 us
    pallas_call x1, Pallas kernels: 95 us -> 71.3 us  [fused_body(): pl.pallas_call(functools.partial(fused_kernel, rows, lead, hidden_units,...]
    unnamed x3 -> x1, local copies, waits for them, and re-layouts: 4.65 us -> 1.67 us
where the time goes in v1:
time: 73.2 us; the launch traced here: 73 us
  Pallas kernels  71.3 us (97%)
  local copies, waits for them, and re-layouts  1.67 us (2%)
    pallas_call x1, Pallas kernels, fused_body(): pl.pallas_call(functools.partial(fused_kernel, rows, lead, hidden_units,...  71.3 us
    unnamed x1, local copies, waits for them, and re-layouts  1.67 us

profile of v1, /device:TPU:0, one launch (start us, length us, event | category | flops | bytes accessed | tf_op | source)
XLA Modules:
  0.0 73.0 jit_solution(15966952434476686066)
XLA Ops:
  0.0 71.3 %shard_map.109 = bf16[128,1024]{1,0:T(8,128)(2,1)} custom-call(bf16[128,1024]{1,0:T(8,128)(2,1)} %tokens_ref.1, f32[1024]{0:T(1024)} %gain_ref.1, bf16[4,1024]{1,0:T(4,128)(2,1)} %bitcast.2, f32[1024]{0:T(1024)} %vector_ref.1, s32[2,128]{1,0:T(2,128)} %bitcast.3, bf16[1,1024,512]{2,1,0:T(8,128)(2,1)} %gate_ref.1, bf16[1,1024,512]{2,1,0:T(8,128)(2,1)} %up_ref.1, ...), custom_call_target="tpu_custom_call" | custom-call | tf_op jit(solution)/shard_map/pallas_call | solution.py:681
  71.3 1.7 %copy.13 = bf16[128,1024]{1,0:T(8,128)(2,1)} copy(bf16[128,1024]{1,0:T(8,128)(2,1)} %shard_map.109) | data formatting | bytes 524288

commit v2 on v1

--- a/solution.py
+++ b/solution.py
@@ -133,31 +133,31 @@
 
 
 ORDER_END = (
-    6, 198, 199, 49, 33, 0, 7, 2, 16, 15, 1, 200, 3, 201, 184, 55, 51, 53, 50, 183, 29, 72, 54,
-    182, 52, 45, 4, 185, 67, 47, 37, 98, 41, 115, 97, 73, 68, 5, 46, 139, 48, 141, 133, 110, 111,
-    75, 158, 140, 142, 176, 153, 134, 99, 118, 177, 96, 159, 154, 160, 171, 173, 175, 163, 167,
-    117, 28, 56, 181, 174, 197, 180, 164, 168, 196, 143, 147, 116, 128, 161, 90, 130, 17, 170,
-    172, 146, 122, 91, 126, 150, 74, 14, 36, 138, 193, 179, 131, 137, 178, 165, 169, 132, 195, 35,
-    112, 113, 114, 40, 192, 44, 155, 157, 156, 34, 85, 87, 88, 194, 127, 129, 89, 30, 31, 32, 95,
-    189, 94, 162, 166, 188, 136, 202, 135, 84, 191, 86, 203, 204, 144, 148, 145, 149, 79, 83, 190,
-    93, 92, 121, 125, 186, 69, 70, 71, 207, 205, 120, 124, 208, 206, 187, 152, 151, 102, 103, 119,
-    13, 106, 123, 100, 104, 101, 77, 12, 105, 107, 81, 78, 82, 209, 76, 80, 108, 10, 57, 61, 58,
-    59, 63, 60, 39, 62, 64, 43, 109, 11, 38, 42, 20, 21, 24, 65, 8, 18, 22, 19, 23, 25, 66, 9, 26,
-    27,
+    6, 198, 199, 49, 33, 0, 7, 2, 15, 17, 1, 200, 201, 3, 184, 55, 51, 53, 50, 37, 41, 182, 29,
+    72, 54, 183, 52, 45, 185, 4, 96, 47, 98, 115, 97, 73, 99, 5, 46, 139, 48, 141, 133, 110, 116,
+    111, 117, 158, 140, 142, 176, 134, 153, 68, 118, 177, 67, 159, 154, 160, 171, 173, 174, 163,
+    167, 14, 16, 181, 197, 180, 128, 130, 131, 196, 122, 161, 90, 126, 75, 56, 138, 193, 143, 147,
+    137, 164, 175, 28, 168, 192, 35, 34, 112, 114, 165, 169, 91, 146, 121, 113, 150, 125, 74, 132,
+    155, 170, 172, 79, 156, 157, 88, 83, 36, 179, 195, 178, 103, 85, 87, 89, 194, 107, 102, 69,
+    70, 127, 129, 202, 95, 189, 94, 120, 124, 71, 188, 203, 144, 148, 136, 135, 145, 162, 149,
+    191, 166, 100, 101, 105, 119, 190, 123, 207, 208, 40, 44, 104, 152, 13, 77, 106, 81, 151, 12,
+    30, 31, 109, 78, 204, 82, 58, 32, 57, 84, 86, 61, 11, 76, 80, 59, 63, 93, 187, 108, 92, 62,
+    60, 205, 39, 10, 43, 64, 38, 206, 42, 20, 21, 186, 25, 65, 18, 22, 19, 8, 23, 24, 209, 66, 9,
+    27, 26,
 )
 ORDER_MID = (
-    12, 227, 226, 10, 104, 88, 0, 2, 13, 11, 71, 70, 1, 14, 16, 3, 228, 229, 28, 26, 106, 105,
-    200, 110, 127, 45, 17, 27, 100, 15, 63, 107, 102, 92, 18, 4, 153, 109, 62, 96, 204, 145, 61,
-    208, 40, 46, 41, 201, 170, 64, 19, 101, 205, 152, 103, 123, 188, 203, 212, 58, 7, 165, 209,
-    154, 146, 48, 60, 50, 202, 189, 213, 54, 49, 6, 166, 122, 187, 198, 53, 57, 9, 211, 59, 30,
-    151, 172, 84, 183, 199, 186, 185, 52, 210, 173, 130, 83, 29, 56, 176, 8, 196, 143, 180, 177,
-    181, 171, 197, 108, 111, 144, 42, 158, 140, 142, 167, 206, 182, 168, 169, 184, 91, 47, 134,
-    207, 138, 193, 225, 128, 69, 72, 129, 139, 5, 141, 192, 194, 224, 124, 175, 179, 162, 195, 43,
-    157, 68, 132, 136, 217, 150, 221, 155, 161, 159, 89, 90, 156, 67, 133, 216, 137, 191, 223,
-    112, 94, 160, 44, 98, 149, 220, 115, 174, 178, 119, 125, 66, 215, 190, 222, 76, 51, 55, 230,
-    131, 126, 231, 34, 135, 31, 32, 33, 65, 214, 93, 232, 97, 148, 35, 219, 36, 114, 95, 99, 147,
-    218, 113, 235, 73, 118, 116, 85, 233, 37, 117, 164, 25, 87, 86, 163, 24, 236, 234, 39, 21,
-    120, 22, 80, 77, 74, 75, 38, 20, 121, 23, 79, 78, 237, 81, 82,
+    12, 227, 10, 226, 104, 88, 0, 13, 2, 11, 70, 71, 1, 14, 3, 16, 229, 228, 110, 26, 106, 105,
+    92, 96, 200, 28, 45, 17, 127, 27, 100, 15, 107, 63, 102, 4, 18, 109, 153, 61, 204, 145, 208,
+    62, 122, 46, 41, 201, 170, 19, 64, 101, 205, 103, 152, 123, 188, 202, 212, 58, 7, 165, 209,
+    146, 111, 60, 49, 6, 198, 213, 189, 53, 57, 166, 40, 186, 130, 59, 50, 9, 210, 199, 54, 83,
+    174, 203, 29, 129, 8, 143, 178, 30, 134, 206, 173, 154, 48, 108, 144, 138, 133, 196, 137, 183,
+    187, 211, 185, 84, 151, 47, 124, 177, 197, 181, 115, 128, 69, 140, 126, 172, 142, 182, 207,
+    184, 193, 225, 167, 168, 171, 169, 91, 52, 5, 194, 56, 192, 224, 176, 195, 180, 72, 125, 89,
+    150, 221, 68, 42, 149, 175, 217, 44, 179, 43, 220, 158, 157, 67, 95, 99, 216, 156, 160, 155,
+    114, 162, 90, 51, 55, 85, 132, 136, 159, 161, 191, 223, 32, 31, 33, 190, 222, 139, 141, 34,
+    112, 36, 113, 94, 98, 230, 66, 215, 131, 231, 119, 116, 135, 65, 214, 76, 148, 219, 93, 118,
+    97, 147, 218, 117, 235, 73, 236, 164, 86, 25, 37, 163, 24, 77, 87, 121, 23, 35, 75, 232, 38,
+    20, 80, 74, 78, 120, 22, 79, 39, 21, 233, 234, 237, 81, 82,
 )
 
 
@@ -196,11 +196,11 @@
     lead,
     hidden_units,
     shared_units,
-    tokens_ref,
-    gain_ref,
-    router_ref,
-    vector_ref,
-    ids_ref,
+    tokens_in,
+    gain_in,
+    router_in,
+    vector_in,
+    ids_in,
     gate_ref,
     up_ref,
     down_ref,
@@ -208,6 +208,11 @@
     sup_ref,
     sdown_ref,
     out_ref,
+    tokens_ref,
+    gain_ref,
+    router_ref,
+    vector_ref,
+    ids_ref,
     sc,
     tok_p,
     tok_q,
@@ -252,6 +257,21 @@
     def _():
         pl.semaphore_signal(barrier, inc=1, device_id=partner["out"], device_id_type=MESH)
 
+    inputs = [
+        pltpu.make_async_copy(there, here, load_sem.at[6 + at])
+        for at, (there, here) in enumerate(
+            (
+                (tokens_in, tokens_ref),
+                (gain_in, gain_ref),
+                (router_in, router_ref),
+                (vector_in, vector_ref),
+                (ids_in, ids_ref),
+            )
+        )
+    ]
+    for load in inputs:
+        load.start()
+
     first = pl.multiple_of(d_at * shared_units, shared_units)
     loads = [
         pltpu.make_async_copy(gate_ref.at[0], w_gate.at[:, pl.ds(0, hidden_units)], load_sem.at[0]),
@@ -275,6 +295,8 @@
     ]
     for load in loads:
         load.start()
+    for load in inputs:
+        load.wait()
 
     floats = tokens_ref[...].astype(jnp.float32)
     mean_square = jnp.mean(floats * floats, axis=-1, keepdims=True)
@@ -681,9 +703,14 @@
     return pl.pallas_call(
         functools.partial(fused_kernel, rows, lead, hidden_units, shared_units),
         out_shape=jax.ShapeDtypeStruct((rows, width), jnp.bfloat16),
-        in_specs=[pl.BlockSpec(memory_space=pltpu.VMEM)] * 5 + [anywhere] * 6,
+        in_specs=[anywhere] * 11,
         out_specs=pl.BlockSpec(memory_space=pltpu.VMEM),
         scratch_shapes=[
+            blocks(rows),
+            pltpu.VMEM(norm_gain.shape, norm_gain.dtype),
+            pltpu.VMEM(router_weight.shape[::-1], router_weight.dtype),
+            pltpu.VMEM(shared_gate_vector.shape, shared_gate_vector.dtype),
+            pltpu.VMEM(expert_ids.shape[::-1], expert_ids.dtype),
             pltpu.VMEM((4, 4, 2, 8, rows), jnp.float32),
             blocks(lead, 4, 4, 2),
             blocks(rest, 4, 4, 2),
@@ -705,7 +732,7 @@
             pltpu.VMEM((units, width), jnp.bfloat16),
             pltpu.SemaphoreType.DMA((SEMAPHORES,)),
             pltpu.SemaphoreType.DMA((SEMAPHORES,)),
-            pltpu.SemaphoreType.DMA((6,)),
+            pltpu.SemaphoreType.DMA((11,)),
         ],
         compiler_params=pltpu.CompilerParams(
             collective_id=0, has_side_effects=True, vmem_limit_bytes=VMEM_LIMIT

time: 73.2 us -> 71.9 us (0.982)
  Pallas kernels: 71.3 us -> 70.1 us
    pallas_call x1, Pallas kernels: 71.3 us -> 70.1 us  [fused_body(): pl.pallas_call(functools.partial(fused_kernel, rows, lead, hidden_units,...]
where the time goes in v2:
time: 71.9 us; the launch traced here: 71.8 us
  Pallas kernels  70.1 us (97%)
  local copies, waits for them, and re-layouts  1.67 us (2%)
    pallas_call x1, Pallas kernels, fused_body(): pl.pallas_call(functools.partial(fused_kernel, rows, lead, hidden_units,...  70.1 us
    unnamed x1, local copies, waits for them, and re-layouts  1.67 us

profile of v2, /device:TPU:0, one launch (start us, length us, event | category | flops | bytes accessed | tf_op | source)
XLA Modules:
  0.0 71.8 jit_solution(12856478339439152562)
XLA Ops:
  0.0 70.1 %shard_map.109 = bf16[128,1024]{1,0:T(8,128)(2,1)} custom-call(bf16[128,1024]{1,0:T(8,128)(2,1)} %tokens_in.1, f32[1024]{0:T(1024)} %gain_in.1, bf16[4,1024]{1,0:T(4,128)(2,1)} %bitcast.2, f32[1024]{0:T(1024)} %vector_in.1, s32[2,128]{1,0:T(2,128)} %bitcast.3, bf16[1,1024,512]{2,1,0:T(8,128)(2,1)} %gate_ref.1, bf16[1,1024,512]{2,1,0:T(8,128)(2,1)} %up_ref.1, ...), custom_call_target="tpu_custom_call" | custom-call | tf_op jit(solution)/shard_map/pallas_call | solution.py:703
  70.1 1.7 %copy.13 = bf16[128,1024]{1,0:T(8,128)(2,1)} copy(bf16[128,1024]{1,0:T(8,128)(2,1)} %shard_map.109) | data formatting | bytes 524288

commit v3 on v2

--- a/solution.py
+++ b/solution.py
@@ -133,31 +133,37 @@
 
 
 ORDER_END = (
-    6, 198, 199, 49, 33, 0, 7, 2, 15, 17, 1, 200, 201, 3, 184, 55, 51, 53, 50, 37, 41, 182, 29,
-    72, 54, 183, 52, 45, 185, 4, 96, 47, 98, 115, 97, 73, 99, 5, 46, 139, 48, 141, 133, 110, 116,
-    111, 117, 158, 140, 142, 176, 134, 153, 68, 118, 177, 67, 159, 154, 160, 171, 173, 174, 163,
-    167, 14, 16, 181, 197, 180, 128, 130, 131, 196, 122, 161, 90, 126, 75, 56, 138, 193, 143, 147,
-    137, 164, 175, 28, 168, 192, 35, 34, 112, 114, 165, 169, 91, 146, 121, 113, 150, 125, 74, 132,
-    155, 170, 172, 79, 156, 157, 88, 83, 36, 179, 195, 178, 103, 85, 87, 89, 194, 107, 102, 69,
-    70, 127, 129, 202, 95, 189, 94, 120, 124, 71, 188, 203, 144, 148, 136, 135, 145, 162, 149,
-    191, 166, 100, 101, 105, 119, 190, 123, 207, 208, 40, 44, 104, 152, 13, 77, 106, 81, 151, 12,
-    30, 31, 109, 78, 204, 82, 58, 32, 57, 84, 86, 61, 11, 76, 80, 59, 63, 93, 187, 108, 92, 62,
-    60, 205, 39, 10, 43, 64, 38, 206, 42, 20, 21, 186, 25, 65, 18, 22, 19, 8, 23, 24, 209, 66, 9,
-    27, 26,
+    6, 49, 198, 199, 33, 0, 15, 7, 2, 16, 1, 200, 3, 201, 184, 55,
+    53, 51, 183, 50, 29, 72, 54, 182, 52, 45, 4, 185, 67, 47, 37, 98,
+    41, 115, 97, 73, 68, 5, 46, 139, 48, 141, 133, 110, 111, 158, 75, 140,
+    142, 176, 153, 134, 99, 118, 177, 96, 159, 154, 160, 171, 173, 175, 163, 167,
+    117, 28, 56, 181, 174, 197, 180, 164, 168, 196, 143, 147, 128, 161, 90, 116,
+    130, 17, 170, 172, 146, 122, 91, 126, 150, 74, 14, 36, 138, 193, 179, 131,
+    137, 178, 165, 169, 195, 35, 112, 113, 132, 114, 40, 192, 44, 155, 157, 156,
+    34, 85, 87, 88, 194, 127, 129, 89, 30, 31, 32, 95, 189, 94, 162, 166,
+    188, 136, 191, 202, 135, 84, 86, 203, 204, 144, 148, 190, 145, 149, 79, 83,
+    93, 92, 121, 125, 186, 69, 70, 71, 207, 120, 103, 205, 124, 208, 206, 187,
+    152, 151, 102, 119, 13, 106, 123, 100, 104, 101, 77, 12, 105, 107, 81, 78,
+    82, 209, 76, 80, 108, 10, 57, 61, 58, 59, 63, 60, 39, 62, 64, 43,
+    109, 11, 38, 42, 20, 21, 24, 65, 8, 18, 22, 19, 23, 25, 66, 9,
+    26, 27,
 )
 ORDER_MID = (
-    12, 227, 10, 226, 104, 88, 0, 13, 2, 11, 70, 71, 1, 14, 3, 16, 229, 228, 110, 26, 106, 105,
-    92, 96, 200, 28, 45, 17, 127, 27, 100, 15, 107, 63, 102, 4, 18, 109, 153, 61, 204, 145, 208,
-    62, 122, 46, 41, 201, 170, 19, 64, 101, 205, 103, 152, 123, 188, 202, 212, 58, 7, 165, 209,
-    146, 111, 60, 49, 6, 198, 213, 189, 53, 57, 166, 40, 186, 130, 59, 50, 9, 210, 199, 54, 83,
-    174, 203, 29, 129, 8, 143, 178, 30, 134, 206, 173, 154, 48, 108, 144, 138, 133, 196, 137, 183,
-    187, 211, 185, 84, 151, 47, 124, 177, 197, 181, 115, 128, 69, 140, 126, 172, 142, 182, 207,
-    184, 193, 225, 167, 168, 171, 169, 91, 52, 5, 194, 56, 192, 224, 176, 195, 180, 72, 125, 89,
-    150, 221, 68, 42, 149, 175, 217, 44, 179, 43, 220, 158, 157, 67, 95, 99, 216, 156, 160, 155,
-    114, 162, 90, 51, 55, 85, 132, 136, 159, 161, 191, 223, 32, 31, 33, 190, 222, 139, 141, 34,
-    112, 36, 113, 94, 98, 230, 66, 215, 131, 231, 119, 116, 135, 65, 214, 76, 148, 219, 93, 118,
-    97, 147, 218, 117, 235, 73, 236, 164, 86, 25, 37, 163, 24, 77, 87, 121, 23, 35, 75, 232, 38,
-    20, 80, 74, 78, 120, 22, 79, 39, 21, 233, 234, 237, 81, 82,
+    227, 12, 226, 10, 104, 88, 0, 2, 13, 11, 71, 70, 1, 14, 3, 228,
+    229, 28, 16, 106, 26, 105, 200, 110, 127, 45, 17, 27, 100, 15, 63, 107,
+    102, 92, 18, 4, 153, 96, 109, 62, 204, 201, 145, 61, 208, 40, 46, 41,
+    170, 64, 19, 101, 205, 152, 103, 123, 188, 203, 212, 58, 7, 165, 209, 154,
+    48, 146, 60, 50, 202, 189, 213, 54, 49, 6, 166, 122, 187, 198, 53, 57,
+    9, 211, 30, 59, 151, 83, 172, 183, 84, 199, 186, 185, 52, 210, 173, 130,
+    29, 56, 176, 8, 196, 180, 177, 181, 171, 197, 108, 111, 144, 143, 42, 158,
+    140, 167, 142, 206, 182, 168, 169, 184, 91, 47, 134, 207, 138, 193, 129, 225,
+    128, 69, 72, 139, 5, 141, 192, 194, 224, 124, 175, 157, 179, 162, 195, 43,
+    132, 136, 68, 217, 150, 221, 155, 161, 159, 89, 90, 156, 67, 133, 216, 137,
+    191, 223, 112, 94, 160, 98, 149, 44, 220, 115, 174, 178, 119, 76, 125, 66,
+    190, 215, 222, 51, 55, 230, 131, 126, 231, 34, 135, 31, 32, 33, 65, 214,
+    93, 232, 97, 148, 35, 219, 36, 114, 95, 99, 147, 218, 113, 235, 73, 118,
+    116, 85, 233, 37, 117, 164, 25, 87, 86, 163, 24, 236, 234, 39, 21, 120,
+    22, 80, 77, 74, 75, 38, 121, 20, 23, 79, 78, 237, 82, 81,
 )
 
 

time: 71.9 us -> 71.5 us (level)
  no operation moved by 1% of the time
where the time goes in v3:
time: 71.5 us; the launch traced here: 71.3 us
  Pallas kernels  69.6 us (97%)
  local copies, waits for them, and re-layouts  1.67 us (2%)
    pallas_call x1, Pallas kernels, fused_body(): pl.pallas_call(functools.partial(fused_kernel, rows, lead, hidden_units,...  69.6 us
    unnamed x1, local copies, waits for them, and re-layouts  1.67 us

profile of v3, /device:TPU:0, one launch (start us, length us, event | category | flops | bytes accessed | tf_op | source)
XLA Modules:
  0.0 71.3 jit_solution(7154355453454165240)
XLA Ops:
  0.0 69.6 %shard_map.109 = bf16[128,1024]{1,0:T(8,128)(2,1)} custom-call(bf16[128,1024]{1,0:T(8,128)(2,1)} %tokens_in.1, f32[1024]{0:T(1024)} %gain_in.1, bf16[4,1024]{1,0:T(4,128)(2,1)} %bitcast.2, f32[1024]{0:T(1024)} %vector_in.1, s32[2,128]{1,0:T(2,128)} %bitcast.3, bf16[1,1024,512]{2,1,0:T(8,128)(2,1)} %gate_ref.1, bf16[1,1024,512]{2,1,0:T(8,128)(2,1)} %up_ref.1, ...), custom_call_target="tpu_custom_call" | custom-call | tf_op jit(solution)/shard_map/pallas_call | solution.py:709
  69.6 1.7 %copy.13 = bf16[128,1024]{1,0:T(8,128)(2,1)} copy(bf16[128,1024]{1,0:T(8,128)(2,1)} %shard_map.109) | data formatting | bytes 524288
